TPU v7x, 32 devices: a whole 2x2x4 slice. The times are simulated.
32 devices in a mesh: groups: 2 (over y), seq: 8 (over z, x), section: 2 (over core).
Axes of the slice: x: 2, y: 2, z: 4, core: 2. Of those that a mesh axis runs over, the one named last changes fastest.
Arguments:
- hidden_in: bfloat16 [4, 8192], P('groups', 'seq'), parts along dimension 0, may hold values from -40 to 40
- norm_gain: bfloat16 [2, 8192], P('section', 'seq'), may hold values from 0.5 to 1.5
- qkv_weight: bfloat16 [2, 8192, 10240], P('section', 'seq'), as said below
- out_weight: bfloat16 [2, 8192, 8192], P('section', None, 'seq'), may hold values from -0.0625 to 0.0625
- memory: bfloat16 [2, 4, 8, 32, 2, 128, 128], P('section', 'groups', None, 'seq'), parts along dimension 1, may hold values from -12 to 12
- lengths: int32 [4], P('groups'), parts along dimension 0, may hold values from 2048 to 4096
- selected: int32 [4, 8, 16], P('groups'), parts along dimension 0, may hold values from 0 to 31, all different within a row
Outputs:
- hidden_out: bfloat16 [2, 4, 8192], P('section', 'groups', 'seq'), parts along dimension 1
- attention: bfloat16 [2, 4, 8192], P('section', 'groups'), parts along dimension 1
There are 2 independent parts, one for each index of `groups`. A program takes and returns all parts, laid end to end along the dimension named above; an argument that names none is the same for every part. Nothing has to cross between parts.
Inputs may be any that keep to these rules, and one draw needn't show every extreme that they name: `selected`: for each sequence and key-value head the 16 block numbers differ. `qkv_weight`: every entry's magnitude is at most 256 / sqrt(8192).
All inputs are finite; a program needn't handle non-finite values.
Results may differ from a plain program's by a relative error of at most 0.025.
The roundings to bfloat16 on the way count: a program that leaves them out, or rounds other values in their place, can miss the bound.
Values may be sent and summed in bfloat16 or wider, within the bound.
A program may use at most 128 MiB of HBM per device.

v0:
```python
import jax
import jax.numpy as jnp
from jax import lax
from jax.sharding import PartitionSpec as P

D = 8192
HEADS = 64
KVH = 8
HEAD = 128
BLOCK = 128
MB = 2
SEQ_MB = 1


EPSILON = 1e-05
FLOOR = -1e30


def passed_along(block, axis, distance):
    devices = range(lax.axis_size(axis))
    route = [(i - distance, i) for i in devices if i - distance in devices]
    return lax.ppermute(block, axis, route)


def project_rows(current, gain_vec, weight_in):
    hidden_wide = current.astype(jnp.float32)
    squares_local = jnp.sum(hidden_wide * hidden_wide, axis=1)
    normed = (hidden_wide * gain_vec).astype(jnp.bfloat16)
    partial_value = jnp.dot(normed, weight_in, preferred_element_type=jnp.float32)
    squares, summed = lax.psum((squares_local, partial_value), "seq")
    projected = (summed * lax.rsqrt(squares / D + EPSILON)[:, None]).astype(jnp.bfloat16)
    return (hidden_wide, projected)


def combine_heads(local_peak, local_total, local_out):
    global_peak = lax.pmax(local_peak, "seq")
    factor = jnp.exp(local_peak - global_peak)
    merged_total, merged_out = lax.psum(
        (local_total * factor, local_out * factor[..., None]), "seq"
    )
    return (global_peak, merged_total, merged_out)


def body(hidden_in, norm_gain, qkv_weight, out_weight, memory, lengths, selected):
    section_count = lax.axis_size("section")
    section_index = lax.axis_index("section")
    shard_index = lax.axis_index("seq")
    width_local = hidden_in.shape[1]
    blocks_local = memory.shape[3]
    heads_total = HEADS * HEAD
    kv_width = KVH * HEAD
    group_size = HEADS // KVH
    score_scale = HEAD ** (-0.5)
    gain_vec = norm_gain[0].astype(jnp.float32)
    weight_in = qkv_weight[0]
    weight_out = out_weight[0]
    memory_local = memory[0]
    block_ids = shard_index * blocks_local + jnp.arange(blocks_local, dtype=jnp.int32)
    offsets = jnp.arange(BLOCK, dtype=jnp.int32)
    positions = (block_ids[:, None] * BLOCK + offsets[None, :]).reshape(blocks_local * BLOCK)
    tick_count = MB + section_count - 1
    hidden_rows = jnp.zeros((MB * SEQ_MB, width_local), jnp.bfloat16)
    attention_rows = jnp.zeros((MB * SEQ_MB, heads_total), jnp.bfloat16)
    incoming = jnp.zeros((SEQ_MB, width_local), jnp.bfloat16)
    for tick_index in range(tick_count):
        batch_index = tick_index - section_index
        active = (batch_index >= 0) & (batch_index < MB)
        batch_index = jnp.clip(batch_index, 0, MB - 1)
        row_start = batch_index * SEQ_MB
        fresh_rows = lax.dynamic_slice_in_dim(hidden_in, row_start, SEQ_MB, 0)
        current = jnp.where(section_index == 0, fresh_rows, incoming)
        hidden_wide, projected = project_rows(current, gain_vec, weight_in)
        queries = (
            projected[:, :heads_total].reshape(SEQ_MB, KVH, group_size, HEAD).astype(jnp.float32)
        )
        new_keys = (
            projected[:, heads_total : heads_total + kv_width]
            .reshape(SEQ_MB, KVH, HEAD)
            .astype(jnp.float32)
        )
        new_values = (
            projected[:, heads_total + kv_width :].reshape(SEQ_MB, KVH, HEAD).astype(jnp.float32)
        )
        cache = lax.dynamic_slice_in_dim(memory_local, row_start, SEQ_MB, 0)
        cache_keys = (
            cache[:, :, :, 0].reshape(SEQ_MB, KVH, blocks_local * BLOCK, HEAD).astype(jnp.float32)
        )
        cache_values = (
            cache[:, :, :, 1].reshape(SEQ_MB, KVH, blocks_local * BLOCK, HEAD).astype(jnp.float32)
        )
        scores = (
            jnp.einsum("bgrd,bgnd->bgrn", queries, cache_keys, precision=lax.Precision.HIGHEST)
            * score_scale
        )
        chosen_ids = lax.dynamic_slice_in_dim(selected, row_start, SEQ_MB, 0)
        chosen = (
            jnp.sum(
                (chosen_ids[:, :, :, None] == block_ids[None, None, None, :]).astype(jnp.int32),
                axis=2,
            )
            > 0
        )
        chosen = jnp.broadcast_to(
            chosen[:, :, :, None], (SEQ_MB, KVH, blocks_local, BLOCK)
        ).reshape(SEQ_MB, KVH, blocks_local * BLOCK)
        seq_limit = lax.dynamic_slice_in_dim(lengths, row_start, SEQ_MB, 0)
        live_mask = chosen & (positions[None, None, :] < seq_limit[:, None, None])
        masked = jnp.where(live_mask[:, :, None, :], scores, FLOOR)
        local_peak = jnp.max(masked, axis=3)
        exponent = jnp.where(live_mask[:, :, None, :], jnp.exp(masked - local_peak[..., None]), 0.0)
        local_total = jnp.sum(exponent, axis=3)
        local_out = jnp.einsum(
            "bgrn,bgnd->bgrd", exponent, cache_values, precision=lax.Precision.HIGHEST
        )
        merged_peak, merged_total, merged_out = combine_heads(local_peak, local_total, local_out)
        own_score = (
            jnp.einsum("bgrd,bgd->bgr", queries, new_keys, precision=lax.Precision.HIGHEST)
            * score_scale
        )
        top_score = jnp.maximum(merged_peak, own_score)
        old_factor = jnp.exp(merged_peak - top_score)
        own_factor = jnp.exp(own_score - top_score)
        denominator = merged_total * old_factor + own_factor
        numerator = (
            merged_out * old_factor[..., None] + own_factor[..., None] * new_values[:, :, None, :]
        )
        attended = (
            (numerator / denominator[..., None]).astype(jnp.bfloat16).reshape(SEQ_MB, heads_total)
        )
        branch = jnp.dot(attended, weight_out, preferred_element_type=jnp.float32)
        new_hidden = (hidden_wide + branch).astype(jnp.bfloat16)
        old_hidden = lax.dynamic_slice_in_dim(hidden_rows, row_start, SEQ_MB, 0)
        hidden_rows = lax.dynamic_update_slice_in_dim(
            hidden_rows, jnp.where(active, new_hidden, old_hidden), row_start, 0
        )
        old_attention = lax.dynamic_slice_in_dim(attention_rows, row_start, SEQ_MB, 0)
        attention_rows = lax.dynamic_update_slice_in_dim(
            attention_rows, jnp.where(active, attended, old_attention), row_start, 0
        )
        if tick_index + 1 < tick_count:
            incoming = passed_along(new_hidden, "section", 1)
    return (hidden_rows[None], attention_rows[None])


def solution(mesh):
    return jax.shard_map(
        body,
        mesh=mesh,
        in_specs=(
            P("groups", "seq"),
            P("section", "seq"),
            P("section", "seq", None),
            P("section", None, "seq"),
            P("section", "groups", None, "seq", None, None, None),
            P("groups"),
            P("groups", None, None),
        ),
        out_specs=(P("section", "groups", "seq"), P("section", "groups", None)),
        check_vma=False,
    )
```

profile of v0, /device:TPU:0, one launch (start us, length us, event | category | flops | bytes accessed | tf_op | source)
XLA Modules:
  0.0 347.8 jit_solution(11380249291135931513)
XLA Ops:
  0.6 1.3 multiply_reduce_fusion.2
  2.0 9.9 %fusion.4 = f32[1,10240]{1,0:T(1,128)S(1)} fusion(bf16[1,1024,10240]{2,1,0:T(8,128)(2,1)} %param.9, bf16[1,1024]{1,0:T(2,128)(2,1)} %param.8, pred[]{:T(512)S(6)} %eq.70, bf16[2,1024]{1,0:T(2,128)(2,1)} %param.7, s32[]{:T(128)S(6)} %min.10), kind=kOutput, calls=%fused_computation.4 | convolution fusion | flops 20976640 | bytes 21018628 | tf_op jit(solution)/shard_map/dot_general | solution.py:29
  11.8 40.3 %all-reduce.5 = (f32[1,10240]{1,0:T(1,128)S(1)}, f32[1]{0:T(128)}) all-reduce(f32[1,10240]{1,0:T(1,128)S(1)} %fusion.4, f32[1]{0:T(128)} %bitcast.6), channel_id=1, replica_groups=mesh['groups'=2,'seq'=8,'section'=2] {'seq'}, use_global_device_ids=true, to_apply=%region_1.2 | all-reduce | flops 10241 | bytes 81928 | tf_op jit(solution)/shard_map/psum | solution.py:30
  52.9 0.1 slice_reduce_fusion.2
  53.0 6.5 %dynamic-slice_bitcast_fusion = (bf16[1,8,4,2,128,128]{5,4,3,2,1,0:T(8,128)(2,1)S(1)}, bf16[1,8,4,2,128,128]{5,4,3,2,1,0:T(8,128)(2,1)S(1)}, bf16[1,8,4,2,128,128]{5,4,3,2,1,0:T(8,128)(2,1)}) fusion(bf16[1,2,8,4,2,128,128]{6,5,4,3,2,1,0:T(8,128)(2,1)} %param.11, s32[]{:T(128)S(6)} %min.12, s32[]{:T(128)S(6)} %min.10, s32[]{:T(128)S(6)} %min.11), kind=kLoop, calls=%fused_computation.12 | loop fusion | bytes 12582924 | tf_op jit(solution)/shard_map/dynamic_slice | solution.py:84
  59.4 1.2 fusion.108
  60.6 0.0 copy-done.9
  60.6 0.6 fusion.109
  61.2 0.0 copy-done.8
  61.2 0.4 convert_reduce_fusion
  61.6 0.1 fusion.61
  61.7 1.9 fusion.90
  63.6 0.1 bitcast_and_fusion.2
  63.7 1.7 fusion.110
  65.4 17.1 %pmax.21 = f32[1,8,8]{2,1,0:T(8,128)S(1)} all-reduce(f32[1,8,8]{2,1,0:T(8,128)S(1)} %bitcast.249), channel_id=1, replica_groups=mesh['groups'=2,'seq'=8,'section'=2] {'seq'}, use_global_device_ids=true, to_apply=%region_5.6 | all-reduce | flops 64 | bytes 512 | tf_op jit(solution)/shard_map/pmax | solution.py:36
  82.5 0.2 fusion.42
  82.7 0.6 fusion.17
  83.3 35.3 %all-reduce.4 = (f32[1,8,8,128]{3,2,1,0:T(8,128)S(1)}, f32[1,8,8]{2,1,0:T(8,128)S(1)}) all-reduce(f32[1,8,8,128]{3,2,1,0:T(8,128)S(1)} %fusion.17, f32[1,8,8]{2,1,0:T(8,128)S(1)} %get-tuple-element.45), channel_id=1, replica_groups=mesh['groups'=2,'seq'=8,'section'=2] {'seq'}, use_global_device_ids=true, to_apply=%region_6.7 | all-reduce | flops 8256 | bytes 66048 | tf_op jit(solution)/shard_map/psum | solution.py:38
  118.6 0.1 select_bitcast_fusion
  118.7 0.0 copy-done.5
  118.8 8.2 %broadcast_select_fusion.6 = (bf16[1,1024]{1,0:T(2,128)(2,1)S(1)}, bf16[1,1024]{1,0:T(2,128)(2,1)S(1)}) fusion(pred[]{:T(512)S(6)} %and.53, bf16[8192,1]{0,1:T(2,128)(2,1)S(1)} %reshape.526, bf16[1,8192,1024]{2,1,0:T(8,128)(2,1)} %param.10, bf16[2,1024]{1,0:T(2,128)(2,1)S(1)} %copy-done.5, s32[]{:T(128)S(6)} %min.10, pred[]{:T(512)S(6)} %eq.70), kind=kOutput, calls=%fused_computation.83 | convolution fusion | flops 16782336 | bytes 16799750 | tf_op jit(solution)/shard_map/dot_general | solution.py:130
  126.9 1.3 collective-permute-start
  128.2 0.0 copy-done
  128.3 1.8 fusion.106
  130.0 0.1 bitcast_and_fusion.1
  130.1 0.1 bitcast_and_fusion
  130.3 0.2 dynamic_update_slice.23
  130.6 0.0 collective-permute-done
  130.6 0.6 multiply_reduce_fusion.1
  131.2 8.4 %fusion.2 = f32[1,10240]{1,0:T(1,128)S(1)} fusion(bf16[1,1024,10240]{2,1,0:T(8,128)(2,1)} %param.9, f32[1,1024]{1,0:T(1,128)S(1)} %get-tuple-element.22, bf16[1,1024]{1,0:T(2,128)(2,1)S(1)} %copy-done.6), kind=kOutput, calls=%fused_computation.2 | convolution fusion | flops 20974592 | bytes 21018624 | tf_op jit(solution)/shard_map/dot_general | solution.py:29
  139.6 34.6 %all-reduce.3 = (f32[1,10240]{1,0:T(1,128)S(1)}, f32[1]{0:T(128)}) all-reduce(f32[1,10240]{1,0:T(1,128)S(1)} %fusion.2, f32[1]{0:T(128)} %bitcast.31), channel_id=1, replica_groups=mesh['groups'=2,'seq'=8,'section'=2] {'seq'}, use_global_device_ids=true, to_apply=%region_10.11 | all-reduce | flops 10241 | bytes 81928 | tf_op jit(solution)/shard_map/psum | solution.py:30
  175.0 0.1 slice_reduce_fusion.1
  175.1 0.1 fusion.58
  175.2 0.5 fusion.111
  175.6 18.0 %pmax.22 = f32[1,8,8]{2,1,0:T(8,128)S(1)} all-reduce(f32[1,8,8]{2,1,0:T(8,128)S(1)} %bitcast.251), channel_id=1, replica_groups=mesh['groups'=2,'seq'=8,'section'=2] {'seq'}, use_global_device_ids=true, to_apply=%region_14.15 | all-reduce | flops 64 | bytes 512 | tf_op jit(solution)/shard_map/pmax | solution.py:36
  193.6 0.2 fusion.43
  193.8 0.6 fusion.16
  194.4 34.4 %all-reduce.2 = (f32[1,8,8,128]{3,2,1,0:T(8,128)S(1)}, f32[1,8,8]{2,1,0:T(8,128)S(1)}) all-reduce(f32[1,8,8,128]{3,2,1,0:T(8,128)S(1)} %fusion.16, f32[1,8,8]{2,1,0:T(8,128)S(1)} %get-tuple-element.40), channel_id=1, replica_groups=mesh['groups'=2,'seq'=8,'section'=2] {'seq'}, use_global_device_ids=true, to_apply=%region_15.16 | all-reduce | flops 8256 | bytes 66048 | tf_op jit(solution)/shard_map/psum | solution.py:38
  228.8 0.1 fusion.125
  228.9 0.1 fusion.123
  229.0 8.0 %broadcast_select_fusion.2 = (bf16[1,1024]{1,0:T(2,128)(2,1)S(1)}, bf16[1,1024]{1,0:T(2,128)(2,1)S(1)}) fusion(pred[]{:T(512)S(6)} %and.56, bf16[2,1024]{1,0:T(2,128)(2,1)S(1)} %dynamic_update_slice.20, s32[]{:T(128)S(6)} %min.11, f32[1,1024]{1,0:T(1,128)S(1)} %get-tuple-element.22, bf16[8192,1]{0,1:T(2,128)(2,1)S(1)} %reshape.532, ...), kind=kOutput, calls=%fused_computation.79 | convolution fusion | flops 16780288 | bytes 16803844 | tf_op jit(solution)/shard_map/dot_general | solution.py:130
  237.1 1.4 collective-permute-start.1
  238.5 0.1 broadcast_select_fusion.1
  238.6 0.2 dynamic_update_slice.24
  238.9 0.4 collective-permute-done.1
  239.3 0.6 multiply_reduce_fusion
  239.9 8.4 %fusion = f32[1,10240]{1,0:T(1,128)S(1)} fusion(bf16[1,1024,10240]{2,1,0:T(8,128)(2,1)} %param.9, f32[1,1024]{1,0:T(1,128)S(1)} %get-tuple-element.20, bf16[1,1024]{1,0:T(2,128)(2,1)S(1)} %copy-done.6), kind=kOutput, calls=%fused_computation | convolution fusion | flops 20974592 | bytes 21018624 | tf_op jit(solution)/shard_map/dot_general | solution.py:29
  248.3 35.3 %all-reduce.1 = (f32[1,10240]{1,0:T(1,128)S(1)}, f32[1]{0:T(128)}) all-reduce(f32[1,10240]{1,0:T(1,128)S(1)} %fusion, f32[1]{0:T(128)} %bitcast.56), channel_id=1, replica_groups=mesh['groups'=2,'seq'=8,'section'=2] {'seq'}, use_global_device_ids=true, to_apply=%region_19.20 | all-reduce | flops 10241 | bytes 81928 | tf_op jit(solution)/shard_map/psum | solution.py:30
  284.4 0.1 slice_reduce_fusion
  284.5 0.1 fusion.55
  284.6 0.0 copy-done.1
  284.6 0.5 fusion.112
  285.1 17.2 %pmax.23 = f32[1,8,8]{2,1,0:T(8,128)S(1)} all-reduce(f32[1,8,8]{2,1,0:T(8,128)S(1)} %bitcast.250), channel_id=1, replica_groups=mesh['groups'=2,'seq'=8,'section'=2] {'seq'}, use_global_device_ids=true, to_apply=%region_23.24 | all-reduce | flops 64 | bytes 512 | tf_op jit(solution)/shard_map/pmax | solution.py:36
  302.3 0.2 fusion.44
  302.5 0.6 fusion.15
  303.1 35.2 %all-reduce = (f32[1,8,8,128]{3,2,1,0:T(8,128)S(1)}, f32[1,8,8]{2,1,0:T(8,128)S(1)}) all-reduce(f32[1,8,8,128]{3,2,1,0:T(8,128)S(1)} %fusion.15, f32[1,8,8]{2,1,0:T(8,128)S(1)} %get-tuple-element.35), channel_id=1, replica_groups=mesh['groups'=2,'seq'=8,'section'=2] {'seq'}, use_global_device_ids=true, to_apply=%region_24.25 | all-reduce | flops 8256 | bytes 66048 | tf_op jit(solution)/shard_map/psum | solution.py:38
  338.3 0.1 fusion.124
  338.4 0.1 fusion.122
  338.5 8.0 %fusion.39 = bf16[1,1,1024]{2,1,0:T(2,128)(2,1)S(1)} fusion(f32[1,1024]{1,0:T(1,128)S(1)} %get-tuple-element.20, bf16[8192,1]{0,1:T(2,128)(2,1)S(1)} %reshape.538, bf16[1,8192,1024]{2,1,0:T(8,128)(2,1)} %param.10, pred[]{:T(512)S(6)} %and.59, bf16[2,1024]{1,0:T(2,128)(2,1)S(1)} %dynamic_update_slice.21, s32[]{:T(128)S(6)} %min.12), kind=kOutput, calls=%fused_computation.34 | convolution fusion | flops 16780288 | bytes 16801796 | tf_op jit(solution)/shard_map/dot_general | solution.py:130
  346.6 0.0 copy-start.7
  346.6 0.1 fusion.54
  346.7 0.2 dynamic_update_slice.25
  346.9 0.3 copy-done.7
  347.2 0.6 copy-done.4
  (38 shorter events, 0.5 us)
Async XLA Ops:
  1.9 58.6 %copy-start.9 = (s32[2]{0:T(128)S(1)}, s32[2]{0:T(128)}, u32[]{:S(2)}) copy-start(s32[2]{0:T(128)} %param.12) | copy-start | bytes 28
  2.0 59.2 %copy-start.8 = (s32[2,8,16]{2,1,0:T(8,128)S(1)}, s32[2,8,16]{2,1,0:T(8,128)}, u32[]{:S(2)}) copy-start(s32[2,8,16]{2,1,0:T(8,128)} %param.13) | copy-start | bytes 3076
  2.0 116.8 %copy-start.5 = (bf16[2,1024]{1,0:T(2,128)(2,1)S(1)}, bf16[2,1024]{1,0:T(2,128)(2,1)}, u32[]{:S(2)}) copy-start(bf16[2,1024]{1,0:T(2,128)(2,1)} %param.7) | copy-start | bytes 12292
  83.3 47.9 %copy-start.6 = (bf16[1,1024]{1,0:T(2,128)(2,1)S(1)}, bf16[1,1024]{1,0:T(2,128)(2,1)}, u32[]{:S(2)}) copy-start(bf16[1,1024]{1,0:T(2,128)(2,1)} %param.8) | copy-start | bytes 6148
  118.6 9.6 %copy-start = (bf16[1,8,4,2,128,128]{5,4,3,2,1,0:T(8,128)(2,1)S(1)}, bf16[1,8,4,2,128,128]{5,4,3,2,1,0:T(8,128)(2,1)}, u32[]{:S(2)}) copy-start(bf16[1,8,4,2,128,128]{5,4,3,2,1,0:T(8,128)(2,1)} %get-tuple-element.25) | copy-start | bytes 6291460
  126.9 3.6 %collective-permute-start = (bf16[1,1024]{1,0:T(2,128)(2,1)S(1)}, bf16[1,1024]{1,0:T(2,128)(2,1)S(1)}, u32[]{:S(2)}, u32[]{:S(2)}) collective-permute-start(bf16[1,1024]{1,0:T(2,128)(2,1)S(1)} %get-tuple-element.59), channel_id=1, source_target_pairs={{0,1},{2,3},{4,5},{6,7},{8,9},{10,11},{12,13},{14,15},{16,17},{18,... | collective-permute-start | bytes 6152 | tf_op jit(solution)/shard_map/ppermute | solution.py:22
  130.0 45.2 %copy-start.3 = (bf16[1,8,4,1,128,128]{5,4,3,2,1,0:T(8,128)(2,1)S(1)}, bf16[1,8,4,1,128,128]{5,4,3,2,1,0:T(8,128)(2,1)}, u32[]{:S(2)}) copy-start(bf16[1,8,4,1,128,128]{5,4,3,2,1,0:T(8,128)(2,1)} %get-tuple-element.67) | copy-start | bytes 3145732
  130.0 63.8 %copy-start.2 = (bf16[1,8,4,1,128,128]{5,4,3,2,1,0:T(8,128)(2,1)S(1)}, bf16[1,8,4,1,128,128]{5,4,3,2,1,0:T(8,128)(2,1)}, u32[]{:S(2)}) copy-start(bf16[1,8,4,1,128,128]{5,4,3,2,1,0:T(8,128)(2,1)} %get-tuple-element.66) | copy-start | bytes 3145732
  237.1 47.6 %copy-start.1 = (bf16[1,8,4,1,128,128]{5,4,3,2,1,0:T(8,128)(2,1)S(1)}, bf16[1,8,4,1,128,128]{5,4,3,2,1,0:T(8,128)(2,1)}, u32[]{:S(2)}) copy-start(bf16[1,8,4,1,128,128]{5,4,3,2,1,0:T(8,128)(2,1)} %get-tuple-element.26) | copy-start | bytes 3145732
  237.1 2.2 collective-permute-start.1
  346.6 0.6 copy-start.7
  347.2 0.6 copy-start.4
where the time goes:
time: 348 us
  blocking collectives  267 us (77%)
  matrix products  55.7 us (16%)
  local copies, waits for them, and re-layouts  12.2 us (4%)
  other arithmetic  6.35 us (2%)
    psum x3, blocking collectives, project_rows(): squares, summed = lax.psum((squares_local, partial_value), 'seq')  110 us
    psum x3, blocking collectives, combine_heads(): lax.psum((local_total * factor, local_out * factor[..., None]), 'seq')  105 us
    pmax x3, blocking collectives, combine_heads(): global_peak = lax.pmax(local_peak, 'seq')  52.3 us
    dot_general x3, matrix products, project_rows(): jnp.dot(normed, weight_in, preferred_element_type=jnp.float32)  26.7 us
    dot_general x3, matrix products, body(): branch = jnp.dot(attended, weight_out, preferred_element_type=jnp.float32)  24.3 us
  transfers between devices with their start and end apart: 2, of which 1 were waited for; matrix products, arithmetic and copies ran while one was open for 1% of the time, Pallas kernels for 0%

commit v1 on v0

v1 whole, which is shorter than its diff:
```python
import functools

import jax
import jax.numpy as jnp
from jax import lax
from jax.experimental import pallas as pl
from jax.experimental.pallas import tpu as pltpu
from jax.sharding import PartitionSpec as P

D = 8192
HEADS = 64
KVH = 8
HEAD = 128
BLOCK = 128
GROUP = HEADS // KVH
GW = GROUP * HEAD
EPSILON = 1e-05
FLOOR = -1e30
MESH = pl.DeviceIdType.MESH


def kernel(
    seq_count,
    section_count,
    hidden_ref,
    gain_ref,
    lengths_ref,
    selected_ref,
    qkv_hbm,
    out_hbm,
    memory_hbm,
    hidden_out,
    attention_out,
    w_q,
    w_kv,
    w_o,
    cache,
    hidden,
    hidden_send,
    live,
    part,
    part_kv,
    got,
    got_kv,
    own_q,
    q_all,
    stats,
    got_stats,
    att_all,
    att_wide,
    w_sem,
    kv_sem,
    o_sem,
    cache_sem,
    hid_sems,
    part_send,
    part_recv,
    partkv_send,
    partkv_recv,
    q_send,
    q_recv,
    st_send,
    st_recv,
    att_send,
    att_recv,
):
    me = lax.axis_index("seq")
    section = lax.axis_index("section")
    ratio = seq_count // KVH
    home = me // ratio
    seqs = hidden_ref.shape[0]
    width = hidden_ref.shape[1]
    blocks_local = memory_hbm.shape[3]
    tokens = blocks_local * BLOCK
    score_scale = HEAD ** (-0.5)
    order = [lax.rem(home + 1 + i, KVH) for i in range(KVH)]

    def when_owner(fn):
        if ratio == 1:
            fn()
        else:
            pl.when(me == home * ratio)(fn)

    def when_not_owner(fn):
        if ratio != 1:
            pl.when(me != home * ratio)(fn)

    def peer(i):
        return lax.rem(me + i, seq_count)

    def remote(src, dst, send, recv, target):
        return pltpu.make_async_remote_copy(
            src_ref=src,
            dst_ref=dst,
            send_sem=send,
            recv_sem=recv,
            device_id={"seq": target},
            device_id_type=MESH,
        )

    w_copies = []
    for i, g in enumerate(order):
        c = pltpu.make_async_copy(
            qkv_hbm.at[0, :, pl.ds(pl.multiple_of(g * GW, GW), GW)], w_q.at[i], w_sem.at[i]
        )
        c.start()
        w_copies.append(c)
    kv_copy = pltpu.make_async_copy(
        qkv_hbm.at[0, :, pl.ds(HEADS * HEAD, 2 * KVH * HEAD)], w_kv, kv_sem
    )
    kv_copy.start()
    cache_copy = pltpu.make_async_copy(memory_hbm.at[0], cache, cache_sem)
    cache_copy.start()
    o_copies = []
    for g in range(KVH):
        o_copies.append(
            pltpu.make_async_copy(out_hbm.at[0, pl.ds(g * GW, GW), :], w_o.at[g], o_sem.at[g])
        )
        o_copies[g].start()

    barrier = pltpu.get_barrier_semaphore()
    for i in range(1, seq_count):
        pl.semaphore_signal(barrier, inc=1, device_id={"seq": peer(i)}, device_id_type=MESH)
    for i in range(1, section_count):
        pl.semaphore_signal(
            barrier,
            inc=1,
            device_id={"section": lax.rem(section + i, section_count)},
            device_id_type=MESH,
        )

    offsets = lax.broadcasted_iota(jnp.int32, (KVH, BLOCK), 1)
    for b in range(seqs):
        ids = selected_ref[b]
        for t in range(blocks_local):
            block = me * blocks_local + t
            hit = jnp.max(jnp.where(ids == block, 1.0, 0.0), axis=1, keepdims=True)
            inside = jnp.where(block * BLOCK + offsets < lengths_ref[b], 1.0, 0.0)
            live[b, :, t * BLOCK : (t + 1) * BLOCK] = hit * inside

    pl.semaphore_wait(barrier, seq_count - 1 + section_count - 1)

    def next_section_copy(target):
        return pltpu.make_async_remote_copy(
            src_ref=hidden_send,
            dst_ref=hidden,
            send_sem=hid_sems.at[0],
            recv_sem=hid_sems.at[1],
            device_id={"section": target},
            device_id_type=MESH,
        )

    @pl.when(section == 0)
    def _():
        hidden[...] = hidden_ref[...].astype(jnp.float32)

    @pl.when(section > 0)
    def _():
        next_section_copy(lax.rem(section + 1, section_count)).wait_recv()

    wide = hidden[...]
    normed = (wide * gain_ref[...].astype(jnp.float32)).astype(jnp.bfloat16)
    squared = wide * wide
    squares = squared[:, :HEAD]
    for t in range(1, width // HEAD):
        squares = squares + squared[:, t * HEAD : (t + 1) * HEAD]

    sends = []
    for i, g in enumerate(order):
        w_copies[i].wait()
        acc = jnp.dot(normed, w_q[i], preferred_element_type=jnp.float32)
        owner = g * ratio

        def store(ref):
            ref[:, :GW] = acc
            ref[:, GW:] = squares

        if i < KVH - 1:
            store(part.at[i])
            c = remote(part.at[i], got.at[me], part_send.at[i], part_recv.at[me], owner)
            c.start()
            sends.append(c)
        else:
            when_owner(functools.partial(store, got.at[me]))

            def send_home():
                store(part.at[i])
                remote(part.at[i], got.at[me], part_send.at[i], part_recv.at[me], owner).start()

            when_not_owner(send_home)

    kv_copy.wait()
    acc_kv = jnp.dot(normed, w_kv[...], preferred_element_type=jnp.float32)
    for g in range(KVH):
        part_kv[g, :, :HEAD] = acc_kv[:, g * HEAD : (g + 1) * HEAD]
        part_kv[g, :, HEAD:] = acc_kv[:, (KVH + g) * HEAD : (KVH + g + 1) * HEAD]
    for i in range(KVH - 1):
        g = order[i]
        c = remote(
            part_kv.at[g], got_kv.at[me], partkv_send.at[i], partkv_recv.at[me], g * ratio
        )
        c.start()
        sends.append(c)

    def kv_home():
        got_kv[me] = part_kv[home]

    def kv_away():
        remote(
            part_kv.at[home],
            got_kv.at[me],
            partkv_send.at[KVH - 1],
            partkv_recv.at[me],
            home * ratio,
        ).start()

    when_owner(kv_home)
    when_not_owner(kv_away)

    def project_own():
        for i in range(1, seq_count):
            s = peer(i)
            remote(part.at[0], got.at[s], part_send.at[0], part_recv.at[s], s).wait_recv()
        total = got[0]
        for s in range(1, seq_count):
            total = total + got[s]
        square_sum = jnp.sum(total[:, GW:], axis=1, keepdims=True)
        scale = lax.rsqrt(square_sum / D + EPSILON)
        projected = (total[:, :GW] * scale).astype(jnp.bfloat16).astype(jnp.float32)
        for h in range(GROUP):
            own_q[pl.ds(h, seqs, stride=GROUP), :] = projected[:, h * HEAD : (h + 1) * HEAD]
        own_q[seqs * GROUP : seqs * GROUP + seqs, :] = jnp.broadcast_to(scale, (seqs, HEAD))
        q_all[home] = own_q[: seqs * GROUP, :].astype(jnp.bfloat16)
        for i in range(1, seq_count):
            remote(
                q_all.at[home], q_all.at[home], q_send.at[i], q_recv.at[home], peer(i)
            ).start()

    when_owner(project_own)

    cache_copy.wait()
    lanes = lax.broadcasted_iota(jnp.int32, (GROUP, HEAD), 1)

    def wait_q(g):
        remote(q_all.at[g], q_all.at[g], q_send.at[0], q_recv.at[g], peer(1)).wait_recv()

    for i, g in enumerate(order):
        if i < KVH - 1:
            wait_q(g)
        else:
            when_not_owner(functools.partial(wait_q, g))
        queries = q_all[g]
        outs, peaks, totals = [], [], []
        for b in range(seqs):
            keys = cache[b, g, :, 0].reshape(tokens, HEAD)
            values = cache[b, g, :, 1].reshape(tokens, HEAD)
            scores = lax.dot_general(
                queries, keys, (((1,), (1,)), ((), ())), preferred_element_type=jnp.float32
            )
            scores = scores[b * GROUP : (b + 1) * GROUP] * score_scale
            alive = live[b, pl.ds(g, 1), :] > 0.5
            masked = jnp.where(alive, scores, FLOOR)
            peak = jnp.max(masked, axis=1, keepdims=True)
            weight = jnp.where(alive, jnp.exp(masked - peak), 0.0)
            high = weight.astype(jnp.bfloat16).astype(jnp.float32)
            both = jnp.concatenate([high, weight - high], axis=0).astype(jnp.bfloat16)
            out = jnp.dot(both, values, preferred_element_type=jnp.float32)
            outs.append(out[:GROUP] + out[GROUP:])
            peaks.append(peak)
            totals.append(jnp.sum(weight, axis=1, keepdims=True))
        packed = jnp.zeros((GROUP, HEAD), jnp.float32)
        for b in range(seqs):
            packed = jnp.where(lanes == 2 * b, peaks[b], packed)
            packed = jnp.where(lanes == 2 * b + 1, totals[b], packed)

        def put(ref):
            for b in range(seqs):
                ref[b] = outs[b]
            ref[seqs] = packed

        def send_stats():
            put(stats.at[i])
            c = remote(stats.at[i], got_stats.at[me], st_send.at[i], st_recv.at[me], g * ratio)
            c.start()
            return c

        if i < KVH - 1:
            sends.append(send_stats())
        else:
            when_owner(functools.partial(put, got_stats.at[me]))
            when_not_owner(lambda: send_stats() and None)

    def finish_own():
        for i in range(1, seq_count):
            s = peer(i)
            remote(
                part_kv.at[0], got_kv.at[s], partkv_send.at[0], partkv_recv.at[s], s
            ).wait_recv()
        new_kv = got_kv[0]
        for s in range(1, seq_count):
            new_kv = new_kv + got_kv[s]
        scale = own_q[seqs * GROUP : seqs * GROUP + seqs, :][:, :1]
        new_kv = (new_kv * scale).astype(jnp.bfloat16).astype(jnp.float32)
        own_scores = []
        for b in range(seqs):
            query = own_q[b * GROUP : (b + 1) * GROUP, :]
            own_scores.append(
                jnp.sum(query * new_kv[b : b + 1, :HEAD], axis=1, keepdims=True) * score_scale
            )
        for i in range(1, seq_count):
            s = peer(i)
            remote(stats.at[0], got_stats.at[s], st_send.at[0], st_recv.at[s], s).wait_recv()
        rows = []
        packed = [got_stats[s, seqs] for s in range(seq_count)]
        for b in range(seqs):
            top = own_scores[b]
            for s in range(seq_count):
                top = jnp.maximum(top, packed[s][:, 2 * b : 2 * b + 1])
            own_weight = jnp.exp(own_scores[b] - top)
            denominator = own_weight
            numerator = own_weight * new_kv[b : b + 1, HEAD:]
            for s in range(seq_count):
                factor = jnp.exp(packed[s][:, 2 * b : 2 * b + 1] - top)
                denominator = denominator + packed[s][:, 2 * b + 1 : 2 * b + 2] * factor
                numerator = numerator + got_stats[s, b] * factor
            rows.append(numerator / denominator)
        att_all[home] = jnp.concatenate(rows, axis=0).astype(jnp.bfloat16)
        for i in range(1, seq_count):
            remote(
                att_all.at[home], att_all.at[home], att_send.at[i], att_recv.at[home], peer(i)
            ).start()

    when_owner(finish_own)

    def wait_att(g):
        remote(att_all.at[g], att_all.at[g], att_send.at[0], att_recv.at[g], peer(1)).wait_recv()

    for g in range(KVH):
        o_copies[g].wait()
    branch = jnp.zeros((seqs, width), jnp.float32)
    for i in range(KVH):
        g = lax.rem(home + i, KVH)
        if i > 0:
            wait_att(g)
        else:
            when_not_owner(functools.partial(wait_att, g))
        att_wide[i] = att_all[g].astype(jnp.float32)
        attended = jnp.concatenate(
            [att_wide[i, pl.ds(h, seqs, stride=GROUP), :] for h in range(GROUP)], axis=1
        ).astype(jnp.bfloat16)
        attention_out[0, :, pl.ds(pl.multiple_of(g * GW, GW), GW)] = attended
        branch = branch + jnp.dot(attended, w_o[g], preferred_element_type=jnp.float32)
    new_hidden = (hidden[...] + branch).astype(jnp.bfloat16)
    hidden_out[0] = new_hidden

    @pl.when(section < section_count - 1)
    def _():
        hidden_send[...] = new_hidden.astype(jnp.float32)
        c = next_section_copy(section + 1)
        c.start()
        c.wait_send()

    for c in sends:
        c.wait_send()

    def drain_owner():
        for i in range(1, seq_count):
            remote(
                q_all.at[home], q_all.at[home], q_send.at[i], q_recv.at[home], peer(i)
            ).wait_send()
            remote(
                att_all.at[home], att_all.at[home], att_send.at[i], att_recv.at[home], peer(i)
            ).wait_send()

    def drain_other():
        last = KVH - 1
        to = home * ratio
        remote(part.at[last], got.at[me], part_send.at[last], part_recv.at[me], to).wait_send()
        remote(
            part_kv.at[home], got_kv.at[me], partkv_send.at[last], partkv_recv.at[me], to
        ).wait_send()
        remote(
            stats.at[last], got_stats.at[me], st_send.at[last], st_recv.at[me], to
        ).wait_send()

    when_owner(drain_owner)
    when_not_owner(drain_other)


def body(hidden_in, norm_gain, qkv_weight, out_weight, memory, lengths, selected):
    seq_count = lax.axis_size("seq")
    section_count = lax.axis_size("section")
    seqs, width = hidden_in.shape
    blocks_local = memory.shape[3]
    dma = pltpu.SemaphoreType.DMA
    vmem = pl.BlockSpec(memory_space=pltpu.VMEM)
    anywhere = pl.BlockSpec(memory_space=pl.ANY)
    return pl.pallas_call(
        functools.partial(kernel, seq_count, section_count),
        out_shape=(
            jax.ShapeDtypeStruct((1, seqs, width), jnp.bfloat16),
            jax.ShapeDtypeStruct((1, seqs, HEADS * HEAD), jnp.bfloat16),
        ),
        in_specs=[
            vmem,
            vmem,
            pl.BlockSpec(memory_space=pltpu.SMEM),
            vmem,
            anywhere,
            anywhere,
            anywhere,
        ],
        out_specs=(vmem, vmem),
        scratch_shapes=[
            pltpu.VMEM((KVH, width, GW), jnp.bfloat16),
            pltpu.VMEM((width, 2 * KVH * HEAD), jnp.bfloat16),
            pltpu.VMEM((KVH, GW, width), jnp.bfloat16),
            pltpu.VMEM((seqs, KVH, blocks_local, 2, BLOCK, HEAD), jnp.bfloat16),
            pltpu.VMEM((seqs, width), jnp.float32),
            pltpu.VMEM((seqs, width), jnp.float32),
            pltpu.VMEM((seqs, KVH, blocks_local * BLOCK), jnp.float32),
            pltpu.VMEM((KVH, seqs, GW + HEAD), jnp.float32),
            pltpu.VMEM((KVH, seqs, 2 * HEAD), jnp.float32),
            pltpu.VMEM((seq_count, seqs, GW + HEAD), jnp.float32),
            pltpu.VMEM((seq_count, seqs, 2 * HEAD), jnp.float32),
            pltpu.VMEM((seqs * GROUP + 8, HEAD), jnp.float32),
            pltpu.VMEM((KVH, seqs * GROUP, HEAD), jnp.bfloat16),
            pltpu.VMEM((KVH, seqs + 1, GROUP, HEAD), jnp.float32),
            pltpu.VMEM((seq_count, seqs + 1, GROUP, HEAD), jnp.float32),
            pltpu.VMEM((KVH, seqs * GROUP, HEAD), jnp.bfloat16),
            pltpu.VMEM((KVH, seqs * GROUP, HEAD), jnp.float32),
            dma((KVH,)),
            dma,
            dma((KVH,)),
            dma,
            dma((2,)),
            dma((KVH,)),
            dma((seq_count,)),
            dma((KVH,)),
            dma((seq_count,)),
            dma((seq_count,)),
            dma((KVH,)),
            dma((KVH,)),
            dma((seq_count,)),
            dma((seq_count,)),
            dma((KVH,)),
        ],
        compiler_params=pltpu.CompilerParams(
            collective_id=0, has_side_effects=True, vmem_limit_bytes=56 * 1024 * 1024
        ),
    )(hidden_in, norm_gain, lengths, selected, qkv_weight, out_weight, memory)


def solution(mesh):
    return jax.shard_map(
        body,
        mesh=mesh,
        in_specs=(
            P("groups", "seq"),
            P("section", "seq"),
            P("section", "seq", None),
            P("section", None, "seq"),
            P("section", "groups", None, "seq", None, None, None),
            P("groups"),
            P("groups", None, None),
        ),
        out_specs=(P("section", "groups", "seq"), P("section", "groups", None)),
        check_vma=False,
    )
```

time: 348 us -> 55.5 us (0.16)
  the two profiles are of different devices: /device:TPU:0 before, /device:TPU:1 now
where the time goes in v1:
time: 55.5 us; the launch traced here: 55.2 us
  Pallas kernels  51.9 us (94%)
  local copies, waits for them, and re-layouts  2.67 us (5%)
  between operations  0.64 us (1%)
    pallas_call x1, Pallas kernels, body(): pl.pallas_call(functools.partial(kernel, seq_count, section_count), out_s...  51.9 us
    unnamed x2, local copies, waits for them, and re-layouts  2.67 us

profile of v1, /device:TPU:1, one launch (start us, length us, event | category | flops | bytes accessed | tf_op | source)
XLA Modules:
  0.0 55.2 jit_solution(16663046279246834781)
XLA Ops:
  0.6 51.9 %shard_map.86 = (bf16[1,2,1024]{2,1,0:T(2,128)(2,1)}, bf16[1,2,8192]{2,1,0:T(2,128)(2,1)}) custom-call(bf16[2,1024]{1,0:T(2,128)(2,1)} %hidden_ref.1, bf16[1,1024]{1,0:T(2,128)(2,1)} %gain_ref.1, s32[2]{0:T(128)} %lengths_ref.1, s32[2,8,16]{2,1,0:T(8,128)} %selected_ref.1, bf16[1,1024,10240]{2,1,0:T(8,128)(2,1)} %qkv_hbm.1, bf16[1,8192,1024]{2,1,0:T(8,128)(2,1)} %out_hbm.1, ...), custom_call_target="tpu_custom_call" | custom-call | tf_op jit(solution)/shard_map/pallas_call | solution.py:398
  52.6 1.3 %copy.11 = bf16[1,2,1024]{2,1,0:T(2,128)(2,1)} copy(bf16[1,2,1024]{2,1,0:T(2,128)(2,1)} %get-tuple-element.4) | data formatting | bytes 8192
  53.8 1.4 %copy.12 = bf16[1,2,8192]{2,1,0:T(2,128)(2,1)} copy(bf16[1,2,8192]{2,1,0:T(2,128)(2,1)} %get-tuple-element.5) | data formatting | bytes 65536

commit v2 on v1

v2 whole, which is shorter than its diff:
```python
import functools

import jax
import jax.numpy as jnp
from jax import lax
from jax.experimental import pallas as pl
from jax.experimental.pallas import tpu as pltpu
from jax.sharding import PartitionSpec as P

D = 8192
HEADS = 64
KVH = 8
HEAD = 128
BLOCK = 128
GROUP = HEADS // KVH
GW = GROUP * HEAD
EPSILON = 1e-05
FLOOR = -1e30
MESH = pl.DeviceIdType.MESH
OWNERS = 4
EACH = KVH // OWNERS
ROUNDS = ((3,), (2, 1), (0,))
OUTPUT_ROUNDS = ((3,), (2,), (1,), (0,))


def kernel(
    seq_count,
    section_count,
    hidden_ref,
    gain_ref,
    lengths_ref,
    selected_ref,
    qkv_hbm,
    out_hbm,
    memory_hbm,
    hidden_out,
    attention_out,
    w_q,
    w_kv,
    w_o,
    cache,
    hidden,
    hidden_send,
    live,
    part,
    part_kv,
    got,
    got_kv,
    own_q,
    q_all,
    stats,
    got_stats,
    att_all,
    att_wide,
    w_sem,
    kv_sem,
    o_sem,
    cache_sem,
    hid_sems,
    part_send,
    part_recv,
    partkv_send,
    partkv_recv,
    q_send,
    q_recv,
    st_send,
    st_recv,
    att_send,
    att_recv,
):
    me = lax.axis_index("seq")
    section = lax.axis_index("section")
    first = seq_count // 2 - OWNERS // 2
    home = lax.rem(me + seq_count - first, seq_count)
    half = me // (seq_count // 2)
    side = lax.rem(me, 2)
    seqs = hidden_ref.shape[0]
    width = hidden_ref.shape[1]
    blocks_local = memory_hbm.shape[3]
    tokens = blocks_local * BLOCK
    score_scale = HEAD ** (-0.5)
    order = [
        2 * (1 - half) + 1 - side,
        2 * (1 - half) + side,
        2 * half + 1 - side,
        2 * half + side,
    ]
    is_owner = home < OWNERS

    def when_owner(fn):
        pl.when(is_owner)(fn)

    def when_not_owner(fn):
        pl.when(home >= OWNERS)(fn)

    def peer(i):
        return lax.rem(me + i, seq_count)

    def remote(src, dst, send, recv, target):
        return pltpu.make_async_remote_copy(
            src_ref=src,
            dst_ref=dst,
            send_sem=send,
            recv_sem=recv,
            device_id={"seq": target},
            device_id_type=MESH,
        )

    w_copies = []
    for i in range(KVH):
        g = order[i // EACH] * EACH + i % EACH
        c = pltpu.make_async_copy(
            qkv_hbm.at[0, :, pl.ds(pl.multiple_of(g * GW, GW), GW)], w_q.at[i], w_sem.at[i]
        )
        c.start()
        w_copies.append(c)
    kv_copy = pltpu.make_async_copy(
        qkv_hbm.at[0, :, pl.ds(HEADS * HEAD, 2 * KVH * HEAD)], w_kv, kv_sem
    )
    kv_copy.start()
    cache_copy = pltpu.make_async_copy(memory_hbm.at[0], cache, cache_sem)
    o_copies = []
    for o in range(OWNERS):
        rows_of = pl.ds(o * EACH * GW, EACH * GW)
        o_copies.append(
            pltpu.make_async_copy(out_hbm.at[0, rows_of, :], w_o.at[o], o_sem.at[o])
        )

    barrier = pltpu.get_barrier_semaphore()
    for i in range(1, seq_count):
        pl.semaphore_signal(barrier, inc=1, device_id={"seq": peer(i)}, device_id_type=MESH)
    for i in range(1, section_count):
        pl.semaphore_signal(
            barrier,
            inc=1,
            device_id={"section": lax.rem(section + i, section_count)},
            device_id_type=MESH,
        )

    offsets = lax.broadcasted_iota(jnp.int32, (KVH, BLOCK), 1)
    for b in range(seqs):
        ids = selected_ref[b]
        for t in range(blocks_local):
            block = me * blocks_local + t
            hit = jnp.max(jnp.where(ids == block, 1.0, 0.0), axis=1, keepdims=True)
            inside = jnp.where(block * BLOCK + offsets < lengths_ref[b], 1.0, 0.0)
            live[b, :, t * BLOCK : (t + 1) * BLOCK] = hit * inside

    pl.semaphore_wait(barrier, seq_count - 1 + section_count - 1)

    def next_section_copy(target):
        return pltpu.make_async_remote_copy(
            src_ref=hidden_send,
            dst_ref=hidden,
            send_sem=hid_sems.at[0],
            recv_sem=hid_sems.at[1],
            device_id={"section": target},
            device_id_type=MESH,
        )

    @pl.when(section == 0)
    def _():
        hidden[...] = hidden_ref[...].astype(jnp.float32)

    @pl.when(section > 0)
    def _():
        next_section_copy(lax.rem(section + 1, section_count)).wait_recv()

    wide = hidden[...]
    normed = (wide * gain_ref[...].astype(jnp.float32)).astype(jnp.bfloat16)
    squared = wide * wide
    squares = squared[:, :HEAD]
    for t in range(1, width // HEAD):
        squares = squares + squared[:, t * HEAD : (t + 1) * HEAD]

    sends = []
    last = OWNERS - 1

    def part_copy(i):
        return remote(
            part.at[i], got.at[me], part_send.at[i], part_recv.at[me], first + order[i]
        )

    for i in range(OWNERS):
        pieces = []
        for j in range(i * EACH, (i + 1) * EACH):
            w_copies[j].wait()
            if j == KVH // 2:
                cache_copy.start()
            if j == KVH - 1:
                for c in o_copies:
                    c.start()
            pieces.append(jnp.dot(normed, w_q[j], preferred_element_type=jnp.float32))

        def store(ref):
            for j in range(EACH):
                ref[:, j * GW : (j + 1) * GW] = pieces[j]
            ref[:, EACH * GW :] = squares

        if i < last:
            store(part.at[i])
            c = part_copy(i)
            c.start()
            sends.append(c)
        else:

            def send_last():
                store(part.at[i])
                part_copy(i).start()

            when_owner(functools.partial(store, got.at[me]))
            when_not_owner(send_last)

    kv_copy.wait()
    acc_kv = jnp.dot(normed, w_kv[...], preferred_element_type=jnp.float32)
    span = EACH * HEAD
    for o in range(OWNERS):
        part_kv[o, :, :span] = acc_kv[:, o * span : (o + 1) * span]
        part_kv[o, :, span:] = acc_kv[:, KVH * HEAD + o * span : KVH * HEAD + (o + 1) * span]

    def kv_part_copy(i):
        return remote(
            part_kv.at[order[i]],
            got_kv.at[me],
            partkv_send.at[i],
            partkv_recv.at[me],
            first + order[i],
        )

    for i in range(last):
        c = kv_part_copy(i)
        c.start()
        sends.append(c)

    def kv_home():
        got_kv[me] = part_kv[order[last]]

    when_owner(kv_home)
    when_not_owner(lambda: kv_part_copy(last).start())

    def project_own():
        for i in range(1, seq_count):
            s = peer(i)
            remote(part.at[0], got.at[s], part_send.at[0], part_recv.at[s], s).wait_recv()
        total = got[0]
        for s in range(1, seq_count):
            total = total + got[s]
        square_sum = jnp.sum(total[:, EACH * GW :], axis=1, keepdims=True)
        scale = lax.rsqrt(square_sum / D + EPSILON)
        projected = (total[:, : EACH * GW] * scale).astype(jnp.bfloat16).astype(jnp.float32)
        for j in range(EACH):
            for h in range(GROUP):
                at = (j * GROUP + h) * HEAD
                own_q[pl.ds(j * seqs * GROUP + h, seqs, stride=GROUP), :] = projected[
                    :, at : at + HEAD
                ]
        q_rows = EACH * seqs * GROUP
        own_q[q_rows : q_rows + seqs, :] = jnp.broadcast_to(scale, (seqs, HEAD))
        q_all[order[last]] = own_q[:q_rows, :].astype(jnp.bfloat16)
        for i in range(1, seq_count):
            remote(
                q_all.at[order[last]], q_all.at[order[last]], q_send.at[i], q_recv.at[order[last]], peer(i)
            ).start()

    when_owner(project_own)

    cache_copy.wait()
    lanes = lax.broadcasted_iota(jnp.int32, (GROUP, HEAD), 1)

    def wait_q(g):
        remote(q_all.at[g], q_all.at[g], q_send.at[0], q_recv.at[g], peer(1)).wait_recv()

    def attend(owners):
        pairs = [(o, j, b) for o in owners for j in range(EACH) for b in range(seqs)]
        all_scores = []
        for o, j, b in pairs:
            queries = q_all[o, j * seqs * GROUP : (j + 1) * seqs * GROUP, :]
            keys = cache[b, o * EACH + j, :, 0].reshape(tokens, HEAD)
            scores = lax.dot_general(
                queries, keys, (((1,), (1,)), ((), ())), preferred_element_type=jnp.float32
            )
            all_scores.append(scores[b * GROUP : (b + 1) * GROUP] * score_scale)
        alive = [live[b, pl.ds(o * EACH + j, 1), :] > 0.5 for o, j, b in pairs]
        masked = [jnp.where(a, x, FLOOR) for a, x in zip(alive, all_scores)]
        peaks = [jnp.max(x, axis=1, keepdims=True) for x in masked]
        weights = [
            jnp.where(a, jnp.exp(x - p), 0.0) for a, x, p in zip(alive, masked, peaks)
        ]
        both = []
        for weight in weights:
            high = weight.astype(jnp.bfloat16).astype(jnp.float32)
            both.append(jnp.concatenate([high, weight - high], axis=0).astype(jnp.bfloat16))
        outs = []
        for (o, j, b), w in zip(pairs, both):
            values = cache[b, o * EACH + j, :, 1].reshape(tokens, HEAD)
            out = jnp.dot(w, values, preferred_element_type=jnp.float32)
            outs.append(out[:GROUP] + out[GROUP:])
        totals = [jnp.sum(weight, axis=1, keepdims=True) for weight in weights]
        n = EACH * seqs
        return [
            (outs[k * n : (k + 1) * n], peaks[k * n : (k + 1) * n], totals[k * n : (k + 1) * n])
            for k in range(len(owners))
        ]

    def put(ref, found):
        packed = jnp.zeros((GROUP, HEAD), jnp.float32)
        outs, peaks, totals = found
        for n in range(EACH * seqs):
            ref[n] = outs[n]
            packed = jnp.where(lanes == 2 * n, peaks[n], packed)
            packed = jnp.where(lanes == 2 * n + 1, totals[n], packed)
        ref[EACH * seqs] = packed

    def stats_copy(i):
        return remote(
            stats.at[i], got_stats.at[me], st_send.at[i], st_recv.at[me], first + order[i]
        )

    for batch in ROUNDS:
        for i in batch:
            if i < last:
                wait_q(order[i])
            else:
                when_not_owner(functools.partial(wait_q, order[i]))
        results = attend([order[i] for i in batch])
        for i, found in zip(batch, results):
            put(stats.at[i], found)
            if i < last:
                c = stats_copy(i)
                c.start()
                sends.append(c)
            else:
                when_not_owner(lambda: stats_copy(last).start())

    def keep_stats():
        got_stats[me] = stats[last]

    when_owner(keep_stats)

    def finish_own():
        for i in range(1, seq_count):
            s = peer(i)
            remote(
                part_kv.at[0], got_kv.at[s], partkv_send.at[0], partkv_recv.at[s], s
            ).wait_recv()
        new_kv = got_kv[0]
        for s in range(1, seq_count):
            new_kv = new_kv + got_kv[s]
        q_rows = EACH * seqs * GROUP
        scale = own_q[q_rows : q_rows + seqs, :][:, :1]
        new_kv = (new_kv * scale).astype(jnp.bfloat16).astype(jnp.float32)
        pairs = [(j, b) for j in range(EACH) for b in range(seqs)]
        own_scores, new_values = [], []
        for j, b in pairs:
            at = (j * seqs + b) * GROUP
            query = own_q[at : at + GROUP, :]
            new_key = new_kv[b : b + 1, j * HEAD : (j + 1) * HEAD]
            own_scores.append(jnp.sum(query * new_key, axis=1, keepdims=True) * score_scale)
            new_values.append(new_kv[b : b + 1, (EACH + j) * HEAD : (EACH + j + 1) * HEAD])
        for i in range(1, seq_count):
            s = peer(i)
            remote(stats.at[0], got_stats.at[s], st_send.at[0], st_recv.at[s], s).wait_recv()
        rows = []
        packed = [got_stats[s, EACH * seqs] for s in range(seq_count)]
        for n in range(EACH * seqs):
            top = own_scores[n]
            for s in range(seq_count):
                top = jnp.maximum(top, packed[s][:, 2 * n : 2 * n + 1])
            own_weight = jnp.exp(own_scores[n] - top)
            denominator = own_weight
            numerator = own_weight * new_values[n]
            for s in range(seq_count):
                factor = jnp.exp(packed[s][:, 2 * n : 2 * n + 1] - top)
                denominator = denominator + packed[s][:, 2 * n + 1 : 2 * n + 2] * factor
                numerator = numerator + got_stats[s, n] * factor
            rows.append(numerator / denominator)
        att_all[order[last]] = jnp.concatenate(rows, axis=0).astype(jnp.bfloat16)
        for i in range(1, seq_count):
            remote(
                att_all.at[order[last]], att_all.at[order[last]], att_send.at[i], att_recv.at[order[last]], peer(i)
            ).start()

    when_owner(finish_own)

    def wait_att(g):
        remote(att_all.at[g], att_all.at[g], att_send.at[0], att_recv.at[g], peer(1)).wait_recv()

    for g in range(OWNERS):
        o_copies[g].wait()
    branch = jnp.zeros((seqs, width), jnp.float32)
    for batch in OUTPUT_ROUNDS:
        for i in batch:
            if i < last:
                wait_att(order[i])
            else:
                when_not_owner(functools.partial(wait_att, order[i]))
        for i in batch:
            att_wide[i] = att_all[order[i]].astype(jnp.float32)
        for i in batch:
            attended = jnp.concatenate(
                [
                    att_wide[i, pl.ds(j * seqs * GROUP + h, seqs, stride=GROUP), :]
                    for j in range(EACH)
                    for h in range(GROUP)
                ],
                axis=1,
            ).astype(jnp.bfloat16)
            at = pl.multiple_of(order[i] * EACH * GW, EACH * GW)
            attention_out[0, :, pl.ds(at, EACH * GW)] = attended
            branch = branch + jnp.dot(
                attended, w_o[order[i]], preferred_element_type=jnp.float32
            )
    new_hidden = (hidden[...] + branch).astype(jnp.bfloat16)
    hidden_out[0] = new_hidden

    @pl.when(section < section_count - 1)
    def _():
        hidden_send[...] = new_hidden.astype(jnp.float32)
        c = next_section_copy(section + 1)
        c.start()
        c.wait_send()

    for c in sends:
        c.wait_send()

    def drain_owner():
        for i in range(1, seq_count):
            remote(
                q_all.at[order[last]], q_all.at[order[last]], q_send.at[i], q_recv.at[order[last]], peer(i)
            ).wait_send()
            remote(
                att_all.at[order[last]], att_all.at[order[last]], att_send.at[i], att_recv.at[order[last]], peer(i)
            ).wait_send()

    def drain_other():
        part_copy(last).wait_send()
        kv_part_copy(last).wait_send()
        stats_copy(last).wait_send()

    when_owner(drain_owner)
    when_not_owner(drain_other)


def hand_on(hidden_ref, attention_ref, hidden_out, attention_out):
    hidden_out[...] = hidden_ref[...]
    attention_out[...] = attention_ref[...]


def body(hidden_in, norm_gain, qkv_weight, out_weight, memory, lengths, selected):
    seq_count = lax.axis_size("seq")
    section_count = lax.axis_size("section")
    seqs, width = hidden_in.shape
    blocks_local = memory.shape[3]
    dma = pltpu.SemaphoreType.DMA
    vmem = pl.BlockSpec(memory_space=pltpu.VMEM)
    anywhere = pl.BlockSpec(memory_space=pl.ANY)
    hidden_out, attention = pl.pallas_call(
        functools.partial(kernel, seq_count, section_count),
        out_shape=(
            jax.ShapeDtypeStruct((1, seqs, width), jnp.bfloat16),
            jax.ShapeDtypeStruct((1, seqs, HEADS * HEAD), jnp.bfloat16),
        ),
        in_specs=[
            vmem,
            vmem,
            pl.BlockSpec(memory_space=pltpu.SMEM),
            vmem,
            anywhere,
            anywhere,
            anywhere,
        ],
        out_specs=(vmem, vmem),
        scratch_shapes=[
            pltpu.VMEM((KVH, width, GW), jnp.bfloat16),
            pltpu.VMEM((width, 2 * KVH * HEAD), jnp.bfloat16),
            pltpu.VMEM((OWNERS, EACH * GW, width), jnp.bfloat16),
            pltpu.VMEM((seqs, KVH, blocks_local, 2, BLOCK, HEAD), jnp.bfloat16),
            pltpu.VMEM((seqs, width), jnp.float32),
            pltpu.VMEM((seqs, width), jnp.float32),
            pltpu.VMEM((seqs, KVH, blocks_local * BLOCK), jnp.float32),
            pltpu.VMEM((OWNERS, seqs, EACH * GW + HEAD), jnp.float32),
            pltpu.VMEM((OWNERS, seqs, 2 * EACH * HEAD), jnp.float32),
            pltpu.VMEM((seq_count, seqs, EACH * GW + HEAD), jnp.float32),
            pltpu.VMEM((seq_count, seqs, 2 * EACH * HEAD), jnp.float32),
            pltpu.VMEM((EACH * seqs * GROUP + 8, HEAD), jnp.float32),
            pltpu.VMEM((OWNERS, EACH * seqs * GROUP, HEAD), jnp.bfloat16),
            pltpu.VMEM((OWNERS, EACH * seqs + 1, GROUP, HEAD), jnp.float32),
            pltpu.VMEM((seq_count, EACH * seqs + 1, GROUP, HEAD), jnp.float32),
            pltpu.VMEM((OWNERS, EACH * seqs * GROUP, HEAD), jnp.bfloat16),
            pltpu.VMEM((OWNERS, EACH * seqs * GROUP, HEAD), jnp.float32),
            dma((KVH,)),
            dma,
            dma((OWNERS,)),
            dma,
            dma((2,)),
            dma((OWNERS,)),
            dma((seq_count,)),
            dma((OWNERS,)),
            dma((seq_count,)),
            dma((seq_count,)),
            dma((OWNERS,)),
            dma((OWNERS,)),
            dma((seq_count,)),
            dma((seq_count,)),
            dma((OWNERS,)),
        ],
        compiler_params=pltpu.CompilerParams(
            collective_id=0, has_side_effects=True, vmem_limit_bytes=56 * 1024 * 1024
        ),
    )(hidden_in, norm_gain, lengths, selected, qkv_weight, out_weight, memory)
    return pl.pallas_call(
        hand_on,
        out_shape=(
            jax.ShapeDtypeStruct(hidden_out.shape, hidden_out.dtype),
            jax.ShapeDtypeStruct(attention.shape, attention.dtype),
        ),
        in_specs=[vmem, vmem],
        out_specs=(vmem, vmem),
    )(hidden_out, attention)


def solution(mesh):
    return jax.shard_map(
        body,
        mesh=mesh,
        in_specs=(
            P("groups", "seq"),
            P("section", "seq"),
            P("section", "seq", None),
            P("section", None, "seq"),
            P("section", "groups", None, "seq", None, None, None),
            P("groups"),
            P("groups", None, None),
        ),
        out_specs=(P("section", "groups", "seq"), P("section", "groups", None)),
        check_vma=False,
    )
```

time: 55.5 us -> 47.7 us (0.86)
  Pallas kernels: 51.9 us -> 46.8 us
  local copies, waits for them, and re-layouts: 2.67 us -> 0 us
    pallas_call x1, Pallas kernels: 51.9 us -> 45.5 us  [body(): pl.pallas_call(functools.partial(kernel, seq_count, section_count), out_s...]
    unnamed x2 -> x0, local copies, waits for them, and re-layouts: 2.67 us -> none
    pallas_call x0 -> x1, Pallas kernels: none -> 1.38 us  [body(): pl.pallas_call(hand_on, out_shape=(jax.ShapeDtypeStruct(hidden_out.shape,...]
where the time goes in v2:
time: 47.7 us; the launch traced here: 47.5 us
  Pallas kernels  46.8 us (98%)
  between operations  0.64 us (1%)
    pallas_call x1, Pallas kernels, body(): pl.pallas_call(functools.partial(kernel, seq_count, section_count), out_s...  45.5 us
    pallas_call x1, Pallas kernels, body(): pl.pallas_call(hand_on, out_shape=(jax.ShapeDtypeStruct(hidden_out.shape,...  1.38 us

profile of v2, /device:TPU:1, one launch (start us, length us, event | category | flops | bytes accessed | tf_op | source)
XLA Modules:
  0.0 47.5 jit_solution(3973820128235244556)
XLA Ops:
  0.6 45.5 %shard_map.86 = (bf16[1,2,1024]{2,1,0:T(2,128)(2,1)}, bf16[1,2,8192]{2,1,0:T(2,128)(2,1)}) custom-call(bf16[2,1024]{1,0:T(2,128)(2,1)} %hidden_ref.1, bf16[1,1024]{1,0:T(2,128)(2,1)} %gain_ref.1, s32[2]{0:T(128)} %lengths_ref.1, s32[2,8,16]{2,1,0:T(8,128)} %selected_ref.1, bf16[1,1024,10240]{2,1,0:T(8,128)(2,1)} %qkv_hbm.1, bf16[1,8192,1024]{2,1,0:T(8,128)(2,1)} %out_hbm.1, ...), custom_call_target="tpu_custom_call" | custom-call | tf_op jit(solution)/shard_map/pallas_call | solution.py:457
  46.1 1.4 %shard_map.87 = (bf16[1,2,1024]{2,1,0:T(2,128)(2,1)}, bf16[1,2,8192]{2,1,0:T(2,128)(2,1)}) custom-call(bf16[1,2,1024]{2,1,0:T(2,128)(2,1)} %get-tuple-element.4.hidden_ref, bf16[1,2,8192]{2,1,0:T(2,128)(2,1)} %get-tuple-element.5.attention_ref), custom_call_target="tpu_custom_call" | custom-call | tf_op jit(solution)/shard_map/pallas_call | solution.py:511
